TPU v7x, 32 devices: a whole 2x2x4 slice. The times are simulated.
32 devices in a mesh: parts: 2 (over x), cluster: 16 (over z, y, core).
Axes of the slice: x: 2, y: 2, z: 4, core: 2. Of those that a mesh axis runs over, the one named last changes fastest.
Arguments:
- queries: float32 [4096, 1024], P(('parts', 'cluster')), parts along dimension 0, may hold values from -1 to 1
- passages: float32 [64, 128, 1024], P(('parts', 'cluster')), parts along dimension 0, may hold values from -6 to 6
- first_blocks: int32 [4096, 4], P(('parts', 'cluster')), parts along dimension 0, may hold values from 0 to 31, all different within a row; in each aligned block of 128 rows (0 to 127, 128 to 255, ...) at most 24 rows name the same one
- followup_blocks: int32 [4096, 4], P(('parts', 'cluster')), parts along dimension 0, may hold values from 0 to 31, all different within a row; in each aligned block of 128 rows (0 to 127, 128 to 255, ...) at most 24 rows name the same one
Outputs:
- expanded: float32 [4096, 1024], P(('parts', 'cluster')), parts along dimension 0
- second_scores: float32 [4096, 4, 128], P(('parts', 'cluster')), parts along dimension 0
There are 2 independent parts, one for each index of `parts`. A program takes and returns all parts, laid end to end along the dimension named above; each array names one. Nothing has to cross between parts.
Inputs may be any that keep to these rules, and one draw needn't show every extreme that they name: `first_blocks`: each row names 4 different blocks; among the queries of one device no block is named more than 24 times, and some block is named exactly 24 times. `followup_blocks`: each row names 4 different blocks; among the queries of one device no block is named more than 24 times, and some block is named exactly 24 times.
All inputs are finite; a program needn't handle non-finite values.
Results may differ from a plain program's by a relative error of at most 0.00014.
Values sent between devices are 32-bit elements; how exact they have to be, the bound alone decides.
A program may use at most 128 MiB of HBM per device.

v0:
```python
import jax
import jax.numpy as jnp
from jax import lax
from jax.sharding import PartitionSpec as P

SOFTMAX_HEAT = 2.0
FEEDBACK = 0.5


def position_targets(block_ids, capacity):
    flat_ids = block_ids.reshape(-1)
    matches = flat_ids[:, None] == flat_ids[None, :]
    positions = jnp.arange(flat_ids.shape[0], dtype=jnp.int32)
    earlier = positions[None, :] < positions[:, None]
    ranking = jnp.sum(jnp.logical_and(matches, earlier), axis=1, dtype=jnp.int32)
    return flat_ids * capacity + ranking


def pack_rows(values, targets, owners, resident_blocks, capacity):
    buffer = jnp.zeros((owners * resident_blocks * capacity, values.shape[1]), values.dtype)
    buffer = buffer.at[targets].set(values)
    return buffer.reshape(owners, resident_blocks, capacity, values.shape[1])


def reply(results):
    return (
        lax.all_to_all(results[0], "cluster", split_axis=0, concat_axis=0, tiled=True),
        lax.all_to_all(results[1], "cluster", split_axis=0, concat_axis=0, tiled=True),
        lax.all_to_all(results[2], "cluster", split_axis=0, concat_axis=0, tiled=True),
    )


def send_back(match_scores):
    return lax.all_to_all(match_scores, "cluster", split_axis=0, concat_axis=0, tiled=True)


def local(queries, passages, first_blocks, followup_blocks):
    owners = lax.axis_size("cluster")
    resident_blocks = passages.shape[0]
    embed_width = queries.shape[1]
    per_query = first_blocks.shape[1]
    pair_count = queries.shape[0] * per_query
    all_blocks = owners * resident_blocks
    capacity = max(2, (3 * pair_count + 2 * all_blocks - 1) // (2 * all_blocks))
    coefficient = FEEDBACK * embed_width ** (-0.5)
    highest = lax.Precision.HIGHEST

    def project_onto_centroid(arrived):
        return jnp.einsum("nbce,bre->nbcr", arrived, passages, precision=highest)

    first_targets = position_targets(first_blocks, capacity)
    second_targets = position_targets(followup_blocks, capacity)
    repeated = jnp.repeat(queries, per_query, axis=0)
    first_sent = pack_rows(repeated, first_targets, owners, resident_blocks, capacity)
    match_scores = SOFTMAX_HEAT * project_onto_centroid(
        lax.all_to_all(first_sent, "cluster", split_axis=0, concat_axis=0, tiled=True)
    )
    highs = jnp.max(match_scores, axis=3)
    weights = jnp.exp(match_scores - highs[..., None])
    totals = jnp.sum(weights, axis=3)
    vectors = jnp.einsum("nbcr,bre->nbce", weights, passages, precision=highest)
    highs, totals, vectors = reply((highs, totals, vectors))
    highs = highs.reshape(-1)[first_targets].reshape(-1, per_query)
    totals = totals.reshape(-1)[first_targets].reshape(-1, per_query)
    vectors = vectors.reshape(-1, embed_width)[first_targets].reshape(-1, per_query, embed_width)
    peak_high = jnp.max(highs, axis=1, keepdims=True)
    scaled = jnp.exp(highs - peak_high)
    denominator = jnp.sum(scaled * totals, axis=1)
    feedback = jnp.einsum("qk,qke->qe", scaled, vectors, precision=highest) / denominator[:, None]
    expanded = queries + coefficient * feedback
    expanded_sent = pack_rows(
        jnp.repeat(expanded, per_query, axis=0), second_targets, owners, resident_blocks, capacity
    )
    returned = (lambda arrived: send_back(project_onto_centroid(arrived)))(
        lax.all_to_all(expanded_sent, "cluster", split_axis=0, concat_axis=0, tiled=True)
    )
    second_scores = returned.reshape(-1, returned.shape[3])[second_targets].reshape(
        queries.shape[0], per_query, -1
    )
    return (expanded, second_scores)


def solution(mesh):
    return jax.shard_map(
        local,
        mesh=mesh,
        in_specs=(
            P(("parts", "cluster"), None),
            P(("parts", "cluster"), None, None),
            P(("parts", "cluster"), None),
            P(("parts", "cluster"), None),
        ),
        out_specs=(P(("parts", "cluster"), None), P(("parts", "cluster"), None, None)),
        check_vma=False,
    )
```

profile of v0, /device:TPU:0, one launch (start us, length us, event | category | flops | bytes accessed | tf_op | source)
XLA Modules:
  0.0 306.5 jit_solution(9194140313527647210)
XLA Ops:
  4.4 1.8 reshape.153
  6.2 5.1 %scatter_custom_fusion = f32[768,1024]{1,0:T(8,128)} fusion(s32[512]{0:T(512)S(1)} %bitcast.44, f32[512,1024]{1,0:T(8,128)} %reshape.153, f32[]{:T(128)} %constant.7.clone.1), kind=kCustom, calls=%fused_computation.13 | custom fusion | bytes 3146240 | tf_op jit(solution)/shard_map/scatter | solution.py:21
  11.3 77.0 %all_to_all.30 = f32[16,2,24,1024]{3,2,1,0:T(8,128)S(1)} all-to-all(f32[16,2,24,1024]{3,2,1,0:T(8,128)} %bitcast.39), channel_id=1, replica_groups=mesh['parts'=2,'cluster'=16] {'cluster'}, dimensions={0} | all-to-all | bytes 6291456 | tf_op jit(solution)/shard_map/all_to_all | solution.py:56
  88.3 2.9 fusion.26
  92.2 5.2 %all-to-all-start.3 = ((f32[16,2,24]{2,1,0:T(2,128)}), f32[16,2,24]{2,1,0:T(2,128)S(1)}, u32[]{:S(2)}, u32[]{:S(2)}) async-start(f32[16,2,24]{2,1,0:T(2,128)} %copy.49), calls=%async_computation.3 | async-start | bytes 32768 | tf_op jit(solution)/shard_map/all_to_all | solution.py:28
  98.0 5.9 %all-to-all-done.3 = f32[16,2,24]{2,1,0:T(2,128)S(1)} async-done(((f32[16,2,24]{2,1,0:T(2,128)}), f32[16,2,24]{2,1,0:T(2,128)S(1)}, u32[]{:S(2)}, u32[]{:S(2)}) %all-to-all-start.3) | async-done | bytes 3104 | tf_op jit(solution)/shard_map/all_to_all | solution.py:28
  103.9 3.5 %all-to-all-start.1 = ((f32[16,2,24]{2,1,0:T(2,128)}), f32[16,2,24]{2,1,0:T(2,128)S(1)}, u32[]{:S(2)}, u32[]{:S(2)}) async-start(f32[16,2,24]{2,1,0:T(2,128)} %copy.47), calls=%async_computation.1 | async-start | bytes 32768 | tf_op jit(solution)/shard_map/all_to_all | solution.py:27
  107.4 2.7 convolution_bitcast_fusion
  110.1 1.9 copy.48
  112.0 1.8 all-to-all-done.1
  113.9 4.7 %all-to-all-start.2 = ((f32[16,2,24,1024]{3,2,1,0:T(8,128)}), f32[16,2,24,1024]{3,2,1,0:T(8,128)}, u32[]{:S(2)}, u32[]{:S(2)}) async-start(f32[16,2,24,1024]{3,2,1,0:T(8,128)} %copy.48), calls=%async_computation.2 | async-start | bytes 6291456 | tf_op jit(solution)/shard_map/all_to_all | solution.py:29
  119.4 2.3 gather_fusion.2
  121.9 2.3 gather_fusion
  124.6 53.0 %all-to-all-done.2 = f32[16,2,24,1024]{3,2,1,0:T(8,128)} async-done(((f32[16,2,24,1024]{3,2,1,0:T(8,128)}), f32[16,2,24,1024]{3,2,1,0:T(8,128)}, u32[]{:S(2)}, u32[]{:S(2)}) %all-to-all-start.2) | async-done | bytes 3145760 | tf_op jit(solution)/shard_map/all_to_all | solution.py:29
  177.6 4.7 %gather_fusion.1 = f32[512,1024]{1,0:T(8,128)S(1)} fusion(f32[768,1024]{1,0:T(8,128)} %bitcast.10, s32[1024]{0:T(1024)S(1)} %pad_clamp_fusion.1), kind=kCustom, calls=%fused_computation.1 | custom fusion | bytes 4196352 | tf_op jit(solution)/shard_map/gather | solution.py:65
  182.3 1.7 reshape.110
  184.0 5.4 %fusion.27 = f32[128,1,1024]{2,1,0:T(1,128)S(1)} fusion(f32[128,4,1]{1,2,0:T(1,128)S(1)} %bitcast.41, f32[128,4,1024]{2,1,0:T(4,128)} %reshape.110), kind=kOutput, calls=%fused_computation.41 | convolution fusion | flops 6291456 | bytes 2623488 | tf_op jit(solution)/shard_map/qk,qke->qe/dot_general | solution.py:69
  192.0 1.8 reshape.161
  193.8 5.1 %scatter_custom_fusion.1 = f32[768,1024]{1,0:T(8,128)} fusion(s32[512]{0:T(512)S(1)} %bitcast.42, f32[512,1024]{1,0:T(8,128)} %reshape.161, f32[]{:T(128)} %constant.7.clone.1), kind=kCustom, calls=%fused_computation.11 | custom fusion | bytes 3146240 | tf_op jit(solution)/shard_map/scatter | solution.py:21
  198.9 85.0 %all_to_all.31 = f32[16,2,24,1024]{3,2,1,0:T(8,128)S(1)} all-to-all(f32[16,2,24,1024]{3,2,1,0:T(8,128)} %bitcast.38), channel_id=1, replica_groups=mesh['parts'=2,'cluster'=16] {'cluster'}, dimensions={0} | all-to-all | bytes 6291456 | tf_op jit(solution)/shard_map/all_to_all | solution.py:75
  283.9 2.8 fusion.8
  287.5 5.2 %all-to-all-start.5 = ((f32[16,2,24,128]{3,2,1,0:T(8,128)}), f32[16,2,24,128]{3,2,1,0:T(8,128)S(1)}, u32[]{:S(2)}, u32[]{:S(2)}) async-start(f32[16,2,24,128]{3,2,1,0:T(8,128)} %copy.53), calls=%async_computation.5 | async-start | bytes 786432 | tf_op jit(solution)/shard_map/all_to_all | solution.py:34
  292.7 12.2 %all-to-all-done.5 = f32[16,2,24,128]{3,2,1,0:T(8,128)S(1)} async-done(((f32[16,2,24,128]{3,2,1,0:T(8,128)}), f32[16,2,24,128]{3,2,1,0:T(8,128)S(1)}, u32[]{:S(2)}, u32[]{:S(2)}) %all-to-all-start.5) | async-done | bytes 393248 | tf_op jit(solution)/shard_map/all_to_all | solution.py:34
  304.9 1.6 gather_fusion.3
  (35 shorter events, 10.1 us)
Async XLA Ops:
  0.6 87.7 %copy-start = (f32[2,128,1024]{2,1,0:T(8,128)S(1)}, f32[2,128,1024]{2,1,0:T(8,128)}, u32[]{:S(2)}) copy-start(f32[2,128,1024]{2,1,0:T(8,128)} %param.5) | copy-start | bytes 3145732
  92.2 11.7 %all-to-all-start.3 = ((f32[16,2,24]{2,1,0:T(2,128)}), f32[16,2,24]{2,1,0:T(2,128)S(1)}, u32[]{:S(2)}, u32[]{:S(2)}) async-start(f32[16,2,24]{2,1,0:T(2,128)} %copy.49), calls=%async_computation.3 | async-start | bytes 32768 | tf_op jit(solution)/shard_map/all_to_all | solution.py:28
  103.9 10.0 %all-to-all-start.1 = ((f32[16,2,24]{2,1,0:T(2,128)}), f32[16,2,24]{2,1,0:T(2,128)S(1)}, u32[]{:S(2)}, u32[]{:S(2)}) async-start(f32[16,2,24]{2,1,0:T(2,128)} %copy.47), calls=%async_computation.1 | async-start | bytes 32768 | tf_op jit(solution)/shard_map/all_to_all | solution.py:27
  112.0 6.5 %copy-start.2 = (s32[128,4]{0,1:T(4,128)S(1)}, s32[128,4]{0,1:T(4,128)}, u32[]{:S(2)}) copy-start(s32[128,4]{0,1:T(4,128)} %param.7) | copy-start | bytes 6148
  113.9 63.7 %all-to-all-start.2 = ((f32[16,2,24,1024]{3,2,1,0:T(8,128)}), f32[16,2,24,1024]{3,2,1,0:T(8,128)}, u32[]{:S(2)}, u32[]{:S(2)}) async-start(f32[16,2,24,1024]{3,2,1,0:T(8,128)} %copy.48), calls=%async_computation.2 | async-start | bytes 6291456 | tf_op jit(solution)/shard_map/all_to_all | solution.py:29
  190.6 0.8 copy-start.1
  287.5 17.4 %all-to-all-start.5 = ((f32[16,2,24,128]{3,2,1,0:T(8,128)}), f32[16,2,24,128]{3,2,1,0:T(8,128)S(1)}, u32[]{:S(2)}, u32[]{:S(2)}) async-start(f32[16,2,24,128]{3,2,1,0:T(8,128)} %copy.53), calls=%async_computation.5 | async-start | bytes 786432 | tf_op jit(solution)/shard_map/all_to_all | solution.py:34
where the time goes:
time: 307 us
  blocking collectives  162 us (53%)
  waiting for transfers between devices  72.8 us (24%)
  local copies, waits for them, and re-layouts  35.3 us (11%)
  starting transfers between devices  18.6 us (6%)
  matrix products  13.8 us (4%)
  other arithmetic  3.08 us (1%)
    all_to_all x1, blocking collectives, local(): lax.all_to_all(expanded_sent, 'cluster', split_axis=0, concat_axis=0, til...  85 us
    all_to_all x1, blocking collectives, local(): lax.all_to_all(first_sent, 'cluster', split_axis=0, concat_axis=0, tiled=...  77 us
    all_to_all x1, waiting for transfers between devices, reply(): lax.all_to_all(results[2], 'cluster', split_axis=0, concat_axis=0, tiled=...  53 us
    all_to_all x1, waiting for transfers between devices, send_back(): lax.all_to_all(match_scores, 'cluster', split_axis=0, concat_axis=0, tile...  12.2 us
    scatter x2, local copies, waits for them, and re-layouts, pack_rows(): buffer = buffer.at[targets].set(values)  10.2 us
  transfers between devices with their start and end apart: 4, of which 4 were waited for; matrix products, arithmetic and copies ran while one was open for 4% of the time, Pallas kernels for 0%

commit v1 on v0

--- a/solution.py
+++ b/solution.py
@@ -1,10 +1,16 @@
+import functools
+
 import jax
 import jax.numpy as jnp
 from jax import lax
+from jax.experimental import pallas as pl
+from jax.experimental.pallas import tpu as pltpu
 from jax.sharding import PartitionSpec as P
 
 SOFTMAX_HEAT = 2.0
 FEEDBACK = 0.5
+MASKED = -1e30
+VMEM_BYTES = 60 * 1024 * 1024
 
 
 def position_targets(block_ids, capacity):
@@ -80,9 +86,227 @@
     return (expanded, second_scores)
 
 
+def dot_nt(a, b):
+    return lax.dot_general(a, b, (((1,), (1,)), ((), ())), preferred_element_type=jnp.float32)
+
+
+def dot_nn(a, b):
+    return lax.dot_general(a, b, (((1,), (0,)), ((), ())), preferred_element_type=jnp.float32)
+
+
+def halves(x):
+    high = x.astype(jnp.bfloat16)
+    return high, (x - high.astype(jnp.float32)).astype(jnp.bfloat16)
+
+
+def ring_kernel(
+    chips, queries, passages, first, followup, expanded, scores,
+    corpus, corpus_hi, corpus_lo, pair, total, chosen, picked,
+    load_sem, send_r, recv_r, send_l, recv_l, send_a, recv_a, send_b, recv_b,
+):
+    me = lax.axis_index("cluster")
+    chip, core = me // 2, me % 2
+    rows, width = queries.shape
+    top = first.shape[1]
+    size = passages.shape[1]
+    half = chips // 2
+    spot = (1 - chip % 2) * (chip // 2) + (chip % 2) * (chips - 1 - chip // 2)
+
+    def chip_at(position):
+        position = (position + chips) % chips
+        late = position // half
+        return (1 - late) * (2 * position) + late * (2 * (chips - 1 - position) + 1)
+
+    right = 2 * chip_at(spot + 1) + core
+    left = 2 * chip_at(spot + chips - 1) + core
+    other = 2 * chip + 1 - core
+
+    def remote(src, dst, send, recv, device):
+        return pltpu.make_async_remote_copy(
+            src_ref=src, dst_ref=dst, send_sem=send, recv_sem=recv,
+            device_id={"cluster": device}, device_id_type=pl.DeviceIdType.MESH,
+        )
+
+    def rightward(step, src):
+        return remote(src, corpus.at[step, 0], send_r.at[step], recv_r.at[step], right)
+
+    def leftward(step, src):
+        return remote(src, corpus.at[step, 1], send_l.at[step], recv_l.at[step], left)
+
+    def across_a(step):
+        return remote(corpus.at[step, 0], corpus.at[step, 2], send_a.at[step], recv_a.at[step], other)
+
+    def across_b(step):
+        return remote(corpus.at[step, 1], corpus.at[step, 3], send_b.at[step], recv_b.at[step], other)
+
+    def blocks_of(step):
+        away = (step + 1) // 2
+        from_left = 2 * chip_at(spot + chips - away)
+        from_right = 2 * chip_at(spot + away)
+        a, b = (step + 1) % 2, step % 2
+        return (
+            (from_left + core) * 2 + a,
+            (from_right + core) * 2 + b,
+            (from_left + 1 - core) * 2 + a,
+            (from_right + 1 - core) * 2 + b,
+        )
+
+    loads = (
+        pltpu.make_async_copy(passages.at[1], corpus.at[0, 0], load_sem.at[0]),
+        pltpu.make_async_copy(passages.at[0], corpus.at[0, 1], load_sem.at[1]),
+    )
+    for load in loads:
+        load.start()
+    barrier = pltpu.get_barrier_semaphore()
+    for device in (right, left, other):
+        pl.semaphore_signal(
+            barrier, inc=1, device_id={"cluster": device}, device_id_type=pl.DeviceIdType.MESH
+        )
+    pl.semaphore_wait(barrier, 3)
+    for load in loads:
+        load.wait()
+    rightward(1, corpus.at[0, 1]).start()
+    leftward(1, corpus.at[0, 0]).start()
+
+    def put_pair(x):
+        high, low = halves(x)
+        pair[pl.ds(0, rows), :] = high
+        pair[pl.ds(rows, rows), :] = low
+
+    put_pair(queries[...])
+    total[...] = jnp.zeros_like(total)
+    for j in range(top):
+        column = followup[:, j : j + 1].astype(jnp.float32)
+        chosen[j] = jnp.broadcast_to(column, (rows, size)).T
+    picked[...] = jnp.zeros_like(picked)
+
+    def first_round(step, carry):
+        peak, norm = carry
+
+        @pl.when(step > 0)
+        def _():
+            rightward(step, corpus.at[step, 0]).wait_recv()
+            leftward(step, corpus.at[step, 1]).wait_recv()
+
+        @pl.when(step < chips - 2)
+        def _():
+            rightward(step + 2, corpus.at[step, 0]).start()
+            leftward(step + 2, corpus.at[step, 1]).start()
+
+        across_a(step).start()
+        across_b(step).start()
+        across_a(step).wait_recv()
+        across_b(step).wait_recv()
+
+        for t in range(4):
+            high, low = halves(corpus[step, t])
+            corpus_hi[step, pl.ds(t * size, size), :] = high
+            corpus_lo[step, pl.ds(t * size, size), :] = low
+        both = dot_nt(pair[...], corpus_hi[step])
+        found = SOFTMAX_HEAT * (
+            both[:rows] + both[rows:] + dot_nt(pair[pl.ds(0, rows), :], corpus_lo[step])
+        )
+        parts, hits = [], []
+        top_score = peak
+        for t, block in enumerate(blocks_of(step)):
+            hit = jnp.max(jnp.where(first[...] == block, 1.0, 0.0), axis=1, keepdims=True) > 0.0
+            part = jnp.where(hit, found[:, t * size : (t + 1) * size], MASKED)
+            top_score = jnp.maximum(top_score, jnp.max(part, axis=1, keepdims=True))
+            parts.append(part)
+            hits.append(hit)
+        shrink = jnp.exp(peak - top_score)
+        weights = jnp.concatenate(
+            [jnp.where(hit, jnp.exp(part - top_score), 0.0) for hit, part in zip(hits, parts)], axis=1
+        )
+        norm = norm * shrink + jnp.sum(weights, axis=1, keepdims=True)
+        high, low = halves(weights)
+        mixed = dot_nn(jnp.concatenate([high, low], axis=0), corpus_hi[step])
+        total[...] = total[...] * shrink + (
+            mixed[:rows] + mixed[rows:] + dot_nn(high, corpus_lo[step])
+        )
+        return top_score, norm
+
+    start = (jnp.full((rows, 1), MASKED, jnp.float32), jnp.zeros((rows, 1), jnp.float32))
+    _, norm = lax.fori_loop(0, chips, first_round, start)
+
+    after = queries[...] + (FEEDBACK * width ** (-0.5)) * (total[...] / norm)
+    expanded[...] = after
+    put_pair(after)
+
+    def second_round(step, carry):
+        both = dot_nt(corpus_hi[step], pair[...])
+        found = both[:, :rows] + both[:, rows:] + dot_nt(corpus_lo[step], pair[pl.ds(0, rows), :])
+        ids = [block.astype(jnp.float32) for block in blocks_of(step)]
+        for j in range(top):
+            names = chosen[j]
+            value = picked[j]
+            for t in range(4):
+                value = jnp.where(names == ids[t], found[t * size : (t + 1) * size, :], value)
+            picked[j] = value
+        return carry
+
+    lax.fori_loop(0, chips, second_round, 0)
+    for j in range(top):
+        scores[:, j, :] = picked[j].T
+
+    def drain(step, carry):
+        @pl.when(step > 0)
+        def _():
+            rightward(step, corpus.at[step, 0]).wait_send()
+            leftward(step, corpus.at[step, 1]).wait_send()
+
+        across_a(step).wait_send()
+        across_b(step).wait_send()
+        return carry
+
+    lax.fori_loop(0, chips, drain, 0)
+
+
+def ring_fits(queries, passages, first_blocks):
+    owners = lax.axis_size("cluster")
+    resident, size, width = passages.shape
+    rows = queries.shape[0]
+    corpus = owners * resident * size * width * 8
+    rest = (5 * rows * width + 3 * first_blocks.shape[1] * rows * size) * 4
+    return owners % 4 == 0 and resident == 2 and corpus + 2 * rest < VMEM_BYTES and rows == size
+
+
+def device_program(queries, passages, first_blocks, followup_blocks):
+    if not ring_fits(queries, passages, first_blocks):
+        return local(queries, passages, first_blocks, followup_blocks)
+    chips = lax.axis_size("cluster") // 2
+    rows, width = queries.shape
+    size = passages.shape[1]
+    top = first_blocks.shape[1]
+    vmem = pl.BlockSpec(memory_space=pltpu.VMEM)
+    return pl.pallas_call(
+        functools.partial(ring_kernel, chips),
+        out_shape=(
+            jax.ShapeDtypeStruct((rows, width), jnp.float32),
+            jax.ShapeDtypeStruct((rows, top, size), jnp.float32),
+        ),
+        in_specs=[vmem, pl.BlockSpec(memory_space=pl.ANY), vmem, vmem],
+        out_specs=(vmem, vmem),
+        scratch_shapes=[
+            pltpu.VMEM((chips, 4, size, width), jnp.float32),
+            pltpu.VMEM((chips, 4 * size, width), jnp.bfloat16),
+            pltpu.VMEM((chips, 4 * size, width), jnp.bfloat16),
+            pltpu.VMEM((2 * rows, width), jnp.bfloat16),
+            pltpu.VMEM((rows, width), jnp.float32),
+            pltpu.VMEM((top, size, rows), jnp.float32),
+            pltpu.VMEM((top, size, rows), jnp.float32),
+            pltpu.SemaphoreType.DMA((2,)),
+        ]
+        + [pltpu.SemaphoreType.DMA((chips,))] * 8,
+        compiler_params=pltpu.CompilerParams(
+            collective_id=0, has_side_effects=True, vmem_limit_bytes=VMEM_BYTES
+        ),
+    )(queries, passages, first_blocks, followup_blocks)
+
+
 def solution(mesh):
     return jax.shard_map(
-        local,
+        device_program,
         mesh=mesh,
         in_specs=(
             P(("parts", "cluster"), None),

time: 307 us -> 102 us (0.33)
  blocking collectives: 162 us -> 0 us
  Pallas kernels: 0 us -> 95.3 us
  waiting for transfers between devices: 72.8 us -> 0 us
  local copies, waits for them, and re-layouts: 35.3 us -> 4.8 us
  starting transfers between devices: 18.6 us -> 0 us
  matrix products: 13.8 us -> 0 us
  other arithmetic: 3.08 us -> 0 us
    all_to_all x2 -> x0, blocking collectives: 162 us -> none  [the longest x1 85 us: local(): lax.all_to_all(expanded_sent, 'cluster', split_axis=0, concat_axis=0, til...]
    pallas_call x0 -> x1, Pallas kernels: none -> 95.3 us  [device_program(): pl.pallas_call(functools.partial(ring_kernel, chips), out_shape=(jax.Shap...]
    all_to_all x4 -> x0, waiting for transfers between devices: 72.8 us -> none  [the longest x1 53 us: reply(): lax.all_to_all(results[2], 'cluster', split_axis=0, concat_axis=0, tiled=...]
    all_to_all x4 -> x0, starting transfers between devices: 18.6 us -> none  [the longest x1 5.22 us: reply(): lax.all_to_all(results[1], 'cluster', split_axis=0, concat_axis=0, tiled=...]
    dot_general x4 -> x0, matrix products: 13.8 us -> none  [the longest x2 5.68 us: project_onto_centroid(): return jnp.einsum('nbce,bre->nbcr', arrived, passages, precision=highest)]
    gather x4 -> x0, local copies, waits for them, and re-layouts: 10.9 us -> none  [the longest x1 4.71 us: local(): vectors.reshape(-1, embed_width)[first_targets]]
    scatter x2 -> x0, local copies, waits for them, and re-layouts: 10.2 us -> none  [pack_rows(): buffer = buffer.at[targets].set(values)]
    reshape x7 -> x0, local copies, waits for them, and re-layouts: 5.57 us -> none  [the longest x1 1.75 us: local(): repeated = jnp.repeat(queries, per_query, axis=0)]
  transfers between devices with their start and end apart: 4 -> 0, of which waited for: 4 -> 0; matrix products, arithmetic and copies ran while one was open for 4% -> 0% of each run, Pallas kernels for 0% -> 0%
where the time goes in v1:
time: 102 us; the launch traced here: 101 us
  Pallas kernels  95.3 us (93%)
  local copies, waits for them, and re-layouts  4.8 us (5%)
    pallas_call x1, Pallas kernels, device_program(): pl.pallas_call(functools.partial(ring_kernel, chips), out_shape=(jax.Shap...  95.3 us
    unnamed x8, local copies, waits for them, and re-layouts  4.8 us

profile of v1, /device:TPU:0, one launch (start us, length us, event | category | flops | bytes accessed | tf_op | source)
XLA Modules:
  0.0 100.8 jit_solution(8944363610895654606)
XLA Ops:
  0.6 0.0 copy-start.1
  0.6 1.4 %copy.6.first = s32[128,4]{1,0:T(8,128)} copy(s32[128,4]{0,1:T(4,128)} %param.6) | data formatting | bytes 4096 | tf_op args[2]
  2.1 0.0 copy-done.1
  2.1 0.7 copy.7.followup
  2.8 95.3 %shard_map.59 = (f32[128,1024]{1,0:T(8,128)}, f32[128,4,128]{2,1,0:T(4,128)}) custom-call(f32[128,1024]{1,0:T(8,128)} %queries.1, f32[2,128,1024]{2,1,0:T(8,128)} %passages.1, s32[128,4]{1,0:T(8,128)} %copy.6.first, s32[128,4]{1,0:T(8,128)} %copy.7.followup), custom_call_target="tpu_custom_call" | custom-call | tf_op jit(solution)/shard_map/pallas_call | solution.py:282
  98.1 0.0 copy-start
  98.1 1.9 %copy.10 = f32[128,1024]{1,0:T(8,128)} copy(f32[128,1024]{1,0:T(8,128)} %get-tuple-element.4) | data formatting | bytes 1048576
  100.1 0.0 copy-done
  100.1 0.7 copy.11
Async XLA Ops:
  0.6 1.4 %copy-start.1 = (s32[128,4]{0,1:T(4,128)S(1)}, s32[128,4]{0,1:T(4,128)}, u32[]{:S(2)}) copy-start(s32[128,4]{0,1:T(4,128)} %param.7) | copy-start | bytes 6148
  98.1 1.9 %copy-start = (f32[128,4,128]{2,1,0:T(4,128)S(1)}, f32[128,4,128]{2,1,0:T(4,128)}, u32[]{:S(2)}) copy-start(f32[128,4,128]{2,1,0:T(4,128)} %get-tuple-element.5) | copy-start | bytes 786436
